TPU v7x, 32 devices: a whole 2x2x4 slice. The times are simulated.
32 devices in a mesh: rep: 4 (over y, x), fsdp: 8 (over z, core).
Axes of the slice: x: 2, y: 2, z: 4, core: 2. Of those that a mesh axis runs over, the one named last changes fastest.
Arguments:
- inputs: bfloat16 [32, 1024, 768], P(('rep', 'fsdp')), may hold values from -6 to 6
- w_query: bfloat16 [768, 768], P('fsdp'), may hold values from -0.21875 to 0.21875
- w_key: bfloat16 [768, 768], P('fsdp'), may hold values from -0.21875 to 0.21875
- w_value: bfloat16 [768, 768], P('fsdp'), may hold values from -0.21875 to 0.21875
- w_out: bfloat16 [768, 768], P('fsdp'), may hold values from -0.875 to 0.875
- w_gate: bfloat16 [768, 2048], P('fsdp'), may hold values from -0.21875 to 0.21875
- w_up: bfloat16 [768, 2048], P('fsdp'), may hold values from -0.21875 to 0.21875
- w_down: bfloat16 [2048, 768], P('fsdp'), may hold values from -0.125 to 0.125
- norm_attn: bfloat16 [768], P('fsdp'), may hold values from 0.25 to 1.75
- norm_ffn: bfloat16 [768], P('fsdp'), may hold values from 0.25 to 1.75
- lengths: int32 [32], P(('rep', 'fsdp')), may hold values from 64 to 1024, as said below
- cotangent: bfloat16 [32, 1024, 768], P(('rep', 'fsdp')), may hold values from -6 to 6
Outputs:
- output: bfloat16 [32, 1024, 768], P(('rep', 'fsdp'))
- grad_input: bfloat16 [32, 1024, 768], P(('rep', 'fsdp'))
- grad_query: float32 [768, 768], P('fsdp')
- grad_key: float32 [768, 768], P('fsdp')
- grad_value: float32 [768, 768], P('fsdp')
- grad_out: float32 [768, 768], P('fsdp')
- grad_gate: float32 [768, 2048], P('fsdp')
- grad_up: float32 [768, 2048], P('fsdp')
- grad_down: float32 [2048, 768], P('fsdp')
- grad_norm_attn: float32 [768], P('fsdp')
- grad_norm_ffn: float32 [768], P('fsdp')
Inputs may be any that keep to these rules, and one draw needn't show every extreme that they name: Tokens at positions lengths[s] and beyond are padding. Some sequence has exactly 1024 valid tokens.
All inputs are finite; a program needn't handle non-finite values.
Results may differ from a plain program's by a relative error of at most 0.018.
Values may be sent and summed in bfloat16 or wider, within the bound.
No kernel may reach another device: no remote copies, remote signals or barrier semaphores. Data moves between devices by JAX's collectives and lax.ppermute only.
A program may use at most 192 MiB of HBM per device.

v0:
```python
import jax
import jax.numpy as jnp
from jax import lax
from jax.sharding import PartitionSpec as P

HEADS = 12


EPSILON = 1e-05


def rotary_tables(seq_length, head_width):
    half_width = head_width // 2
    position = jnp.arange(seq_length, dtype=jnp.float32)
    inverse = 10000.0 ** (-(jnp.arange(half_width, dtype=jnp.float32) * 2.0 / head_width))
    angles = position[:, None] * inverse[None, :]
    return (jnp.cos(angles)[:, None, :], jnp.sin(angles)[:, None, :])


def rotate(values, cosine, sine_table):
    half_width = values.shape[-1] // 2
    former = values[..., :half_width]
    latter = values[..., half_width:]
    return jnp.concatenate(
        [former * cosine - latter * sine_table, latter * cosine + former * sine_table], axis=-1
    )


def unrotate(grads_in, cosine, sine_table):
    half_width = grads_in.shape[-1] // 2
    former = grads_in[..., :half_width]
    latter = grads_in[..., half_width:]
    return jnp.concatenate(
        [former * cosine + latter * sine_table, latter * cosine - former * sine_table], axis=-1
    )


def rms_parts(values):
    inv_rms = lax.rsqrt(jnp.mean(values * values, axis=-1, keepdims=True) + EPSILON)
    return (values * inv_rms, inv_rms)


def norm_back(grad_normed, normed, inv_rms, gain):
    grad_gain = jnp.sum(grad_normed * normed, axis=0)
    scaled = grad_normed * gain
    return (
        inv_rms * (scaled - normed * jnp.mean(scaled * normed, axis=-1, keepdims=True)),
        grad_gain,
    )


def local(
    inputs,
    w_query,
    w_key,
    w_value,
    w_out,
    w_gate,
    w_up,
    w_down,
    norm_attn,
    norm_ffn,
    lengths,
    cotangent,
):
    gathered = (
        lax.all_gather(w_query, "fsdp", axis=0, tiled=True),
        lax.all_gather(w_key, "fsdp", axis=0, tiled=True),
        lax.all_gather(w_value, "fsdp", axis=0, tiled=True),
        lax.all_gather(w_out, "fsdp", axis=0, tiled=True),
        lax.all_gather(w_gate, "fsdp", axis=0, tiled=True),
        lax.all_gather(w_up, "fsdp", axis=0, tiled=True),
        lax.all_gather(w_down, "fsdp", axis=0, tiled=True),
        lax.all_gather(norm_attn, "fsdp", axis=0, tiled=True),
        lax.all_gather(norm_ffn, "fsdp", axis=0, tiled=True),
    )
    seq_count, seq_length, model_width = inputs.shape
    head_count = HEADS
    head_width = model_width // head_count
    row_count = seq_count * seq_length
    score_scale = head_width ** (-0.5)
    cosine, sine_table = rotary_tables(seq_length, head_width)
    position = jnp.arange(seq_length, dtype=jnp.int32)
    allowed = (position[None, None, :] <= position[None, :, None]) & (
        position[None, None, :] < lengths[:, None, None]
    )
    shape_heads = (seq_count, seq_length, head_count, head_width)

    def split_heads(values):
        return values.reshape(shape_heads).transpose(2, 0, 1, 3)

    def join_heads(values):
        return values.transpose(1, 2, 0, 3)

    inputs_f = inputs.reshape(row_count, model_width).astype(jnp.float32)
    normed_one, inv_one = rms_parts(inputs_f)
    gain_attn = gathered[7].astype(jnp.float32)
    gain_ffn = gathered[8].astype(jnp.float32)
    h_attn = (normed_one * gain_attn).astype(jnp.bfloat16)
    query_raw = jnp.dot(h_attn, gathered[0], preferred_element_type=jnp.float32)
    key_raw = jnp.dot(h_attn, gathered[1], preferred_element_type=jnp.float32)
    query_heads = split_heads(
        rotate(query_raw.reshape(shape_heads), cosine, sine_table)
        .astype(jnp.bfloat16)
        .reshape(row_count, model_width)
    )
    key_heads = split_heads(
        rotate(key_raw.reshape(shape_heads), cosine, sine_table)
        .astype(jnp.bfloat16)
        .reshape(row_count, model_width)
    )
    value_heads = split_heads(
        jnp.dot(h_attn, gathered[2], preferred_element_type=jnp.float32).astype(jnp.bfloat16)
    )

    def head_forward(operands):
        query_head, key_head, value_head = operands
        scores = (
            jnp.einsum("sqe,ske->sqk", query_head, key_head, preferred_element_type=jnp.float32)
            * score_scale
        )
        scores = jnp.where(allowed, scores, -1e30)
        row_max = jnp.max(scores, axis=-1, keepdims=True)
        exponent = jnp.exp(scores - row_max)
        row_sum = jnp.sum(exponent, axis=-1, keepdims=True)
        attention = (exponent / row_sum).astype(jnp.bfloat16)
        mixed = jnp.einsum(
            "sqk,ske->sqe", attention, value_head, preferred_element_type=jnp.float32
        )
        return (mixed, (row_max + jnp.log(row_sum))[..., 0])

    mixed_heads, log_sums = lax.map(head_forward, (query_heads, key_heads, value_heads))
    mixed_rows = join_heads(mixed_heads.astype(jnp.bfloat16)).reshape(row_count, model_width)
    residual = inputs_f + jnp.dot(mixed_rows, gathered[3], preferred_element_type=jnp.float32)
    normed_two, inv_two = rms_parts(residual)
    h_ffn = (normed_two * gain_ffn).astype(jnp.bfloat16)
    gate_proj = jnp.dot(h_ffn, gathered[4], preferred_element_type=jnp.float32)
    up_proj = jnp.dot(h_ffn, gathered[5], preferred_element_type=jnp.float32)
    sigmoid_gate = jax.nn.sigmoid(gate_proj)
    silu_gate = gate_proj * sigmoid_gate
    hidden = (silu_gate * up_proj).astype(jnp.bfloat16)
    ffn_out = jnp.dot(hidden, gathered[6], preferred_element_type=jnp.float32)
    output = (residual + ffn_out).astype(jnp.bfloat16).reshape(seq_count, seq_length, model_width)
    weights_bk = (
        lax.all_gather(w_query, "fsdp", axis=0, tiled=True),
        lax.all_gather(w_key, "fsdp", axis=0, tiled=True),
        lax.all_gather(w_value, "fsdp", axis=0, tiled=True),
        lax.all_gather(w_out, "fsdp", axis=0, tiled=True),
        lax.all_gather(w_gate, "fsdp", axis=0, tiled=True),
        lax.all_gather(w_up, "fsdp", axis=0, tiled=True),
        lax.all_gather(w_down, "fsdp", axis=0, tiled=True),
        lax.all_gather(norm_attn, "fsdp", axis=0, tiled=True),
        lax.all_gather(norm_ffn, "fsdp", axis=0, tiled=True),
    )
    valid_rows = (position[None, :] < lengths[:, None]).astype(jnp.float32).reshape(row_count, 1)
    grad_output = cotangent.reshape(row_count, model_width).astype(jnp.float32) * valid_rows
    grad_out_b = grad_output.astype(jnp.bfloat16)
    grad_down = jnp.einsum("rf,rd->fd", hidden, grad_out_b, preferred_element_type=jnp.float32)
    grad_hidden = jnp.einsum(
        "rd,fd->rf", grad_out_b, weights_bk[6], preferred_element_type=jnp.float32
    )
    grad_gate_b = (
        grad_hidden * up_proj * sigmoid_gate * (1.0 + gate_proj * (1.0 - sigmoid_gate))
    ).astype(jnp.bfloat16)
    grad_up_b = (grad_hidden * silu_gate).astype(jnp.bfloat16)
    grad_gate = jnp.einsum("rd,rf->df", h_ffn, grad_gate_b, preferred_element_type=jnp.float32)
    grad_up = jnp.einsum("rd,rf->df", h_ffn, grad_up_b, preferred_element_type=jnp.float32)
    grad_h_ffn = jnp.einsum(
        "rf,df->rd", grad_gate_b, weights_bk[4], preferred_element_type=jnp.float32
    )
    grad_h_ffn = grad_h_ffn + jnp.einsum(
        "rf,df->rd", grad_up_b, weights_bk[5], preferred_element_type=jnp.float32
    )
    grad_res_norm, grad_norm_ffn = norm_back(
        grad_h_ffn, normed_two, inv_two, weights_bk[8].astype(jnp.float32)
    )
    grad_residual = grad_output + grad_res_norm
    grad_attn_b = grad_residual.astype(jnp.bfloat16)
    grad_out = jnp.einsum("rd,re->de", mixed_rows, grad_attn_b, preferred_element_type=jnp.float32)
    grad_mixed = jnp.einsum(
        "re,de->rd", grad_attn_b, weights_bk[3], preferred_element_type=jnp.float32
    ).astype(jnp.bfloat16)
    grad_mixed_heads = split_heads(grad_mixed)

    def head_backward(operands):
        query_head, key_head, value_head, grad_head, log_head = operands
        scores = (
            jnp.einsum("sqe,ske->sqk", query_head, key_head, preferred_element_type=jnp.float32)
            * score_scale
        )
        scores = jnp.where(allowed, scores, -1e30)
        attention = jnp.exp(scores - log_head[..., None])
        attention_b = attention.astype(jnp.bfloat16)
        grad_attention = jnp.einsum(
            "sqe,ske->sqk", grad_head, value_head, preferred_element_type=jnp.float32
        )
        grad_scores = (
            attention
            * (grad_attention - jnp.sum(attention * grad_attention, axis=-1, keepdims=True))
        ).astype(jnp.bfloat16)
        grad_query_head = (
            jnp.einsum("sqk,ske->sqe", grad_scores, key_head, preferred_element_type=jnp.float32)
            * score_scale
        )
        grad_key_head = (
            jnp.einsum("sqk,sqe->ske", grad_scores, query_head, preferred_element_type=jnp.float32)
            * score_scale
        )
        grad_value_head = jnp.einsum(
            "sqk,sqe->ske", attention_b, grad_head, preferred_element_type=jnp.float32
        )
        return (grad_query_head, grad_key_head, grad_value_head)

    grad_q_heads, grad_k_heads, grad_v_heads = lax.map(
        head_backward, (query_heads, key_heads, value_heads, grad_mixed_heads, log_sums)
    )
    grad_q_rows = (
        unrotate(join_heads(grad_q_heads), cosine, sine_table)
        .reshape(row_count, model_width)
        .astype(jnp.bfloat16)
    )
    grad_k_rows = (
        unrotate(join_heads(grad_k_heads), cosine, sine_table)
        .reshape(row_count, model_width)
        .astype(jnp.bfloat16)
    )
    grad_v_rows = join_heads(grad_v_heads).reshape(row_count, model_width).astype(jnp.bfloat16)
    grad_query = jnp.einsum("rd,re->de", h_attn, grad_q_rows, preferred_element_type=jnp.float32)
    grad_key = jnp.einsum("rd,re->de", h_attn, grad_k_rows, preferred_element_type=jnp.float32)
    grad_value = jnp.einsum("rd,re->de", h_attn, grad_v_rows, preferred_element_type=jnp.float32)
    grad_h_attn = jnp.einsum(
        "re,de->rd", grad_q_rows, weights_bk[0], preferred_element_type=jnp.float32
    )
    grad_h_attn = grad_h_attn + jnp.einsum(
        "re,de->rd", grad_k_rows, weights_bk[1], preferred_element_type=jnp.float32
    )
    grad_h_attn = grad_h_attn + jnp.einsum(
        "re,de->rd", grad_v_rows, weights_bk[2], preferred_element_type=jnp.float32
    )
    grad_in_norm, grad_norm_attn = norm_back(
        grad_h_attn, normed_one, inv_one, weights_bk[7].astype(jnp.float32)
    )
    grad_input = (
        (grad_residual + grad_in_norm)
        .astype(jnp.bfloat16)
        .reshape(seq_count, seq_length, model_width)
    )
    owned = (
        lax.psum_scatter(grad_query, "fsdp", scatter_dimension=0, tiled=True),
        lax.psum_scatter(grad_key, "fsdp", scatter_dimension=0, tiled=True),
        lax.psum_scatter(grad_value, "fsdp", scatter_dimension=0, tiled=True),
        lax.psum_scatter(grad_out, "fsdp", scatter_dimension=0, tiled=True),
        lax.psum_scatter(grad_gate, "fsdp", scatter_dimension=0, tiled=True),
        lax.psum_scatter(grad_up, "fsdp", scatter_dimension=0, tiled=True),
        lax.psum_scatter(grad_down, "fsdp", scatter_dimension=0, tiled=True),
        lax.psum_scatter(grad_norm_attn, "fsdp", scatter_dimension=0, tiled=True),
        lax.psum_scatter(grad_norm_ffn, "fsdp", scatter_dimension=0, tiled=True),
    )
    reduced = (
        lax.psum(owned[0].astype(jnp.bfloat16), "rep").astype(jnp.float32),
        lax.psum(owned[1].astype(jnp.bfloat16), "rep").astype(jnp.float32),
        lax.psum(owned[2].astype(jnp.bfloat16), "rep").astype(jnp.float32),
        lax.psum(owned[3].astype(jnp.bfloat16), "rep").astype(jnp.float32),
        lax.psum(owned[4].astype(jnp.bfloat16), "rep").astype(jnp.float32),
        lax.psum(owned[5].astype(jnp.bfloat16), "rep").astype(jnp.float32),
        lax.psum(owned[6].astype(jnp.bfloat16), "rep").astype(jnp.float32),
        lax.psum(owned[7].astype(jnp.bfloat16), "rep").astype(jnp.float32),
        lax.psum(owned[8].astype(jnp.bfloat16), "rep").astype(jnp.float32),
    )
    return (
        output,
        grad_input,
        reduced[0],
        reduced[1],
        reduced[2],
        reduced[3],
        reduced[4],
        reduced[5],
        reduced[6],
        reduced[7],
        reduced[8],
    )


def solution(mesh):
    return jax.shard_map(
        local,
        mesh=mesh,
        in_specs=(
            P(("rep", "fsdp"), None, None),
            P("fsdp", None),
            P("fsdp", None),
            P("fsdp", None),
            P("fsdp", None),
            P("fsdp", None),
            P("fsdp", None),
            P("fsdp", None),
            P("fsdp"),
            P("fsdp"),
            P(("rep", "fsdp")),
            P(("rep", "fsdp"), None, None),
        ),
        out_specs=(
            P(("rep", "fsdp"), None, None),
            P(("rep", "fsdp"), None, None),
            P("fsdp", None),
            P("fsdp", None),
            P("fsdp", None),
            P("fsdp", None),
            P("fsdp", None),
            P("fsdp", None),
            P("fsdp", None),
            P("fsdp"),
            P("fsdp"),
        ),
        check_vma=False,
    )
```

profile of v0, /device:TPU:0, one launch (start us, length us, event | category | flops | bytes accessed | tf_op | source)
XLA Modules:
  0.0 832.0 jit_solution(13768503767765881324)
XLA Ops:
  16.6 18.5 %all-reduce.5 = (bf16[768]{0:T(1024)(128)(2,1)S(1)}, bf16[768]{0:T(1024)(128)(2,1)S(1)}) all-reduce(bf16[768]{0:T(1024)(128)(2,1)S(1)} %dynamic-update-slice, bf16[768]{0:T(1024)(128)(2,1)S(1)} %dynamic-update-slice.1), channel_id=1, replica_groups=mesh['rep'=4,'fsdp'=8] {'fsdp'}, use_global_device_ids=true, to_apply=%add | all-reduce | flops 1536 | bytes 6144
  40.6 18.7 %all-gather.8.cloned.1.call-done = bf16[768,768]{1,0:T(8,128)(2,1)} async-done(((bf16[96,768]{1,0:T(8,128)(2,1)}), bf16[768,768]{1,0:T(8,128)(2,1)}) %all-gather.8.cloned.1.call-update) | async-done | bytes 1179664 | tf_op jit(solution)/shard_map/all_gather | solution.py:67
  67.3 4.1 copy.51
  74.2 9.2 %all-gather.12.cloned.1.call-done = bf16[768,768]{1,0:T(8,128)(2,1)} async-done(((bf16[96,768]{1,0:T(8,128)(2,1)}), bf16[768,768]{1,0:T(8,128)(2,1)}) %all-gather.12.cloned.1.call-update) | async-done | bytes 1179664 | tf_op jit(solution)/shard_map/all_gather | solution.py:69
  83.4 3.9 convolution_convert_fusion.1
  87.3 4.2 copy.50
  91.6 68.2 %while.30 = (s32[]{:T(128)}, bf16[12,1,1024,64]{2,3,1,0:T(8,128)(2,1)S(1)}, f32[12,1,1024]{2,1,0:T(1,128)S(1)}, bf16[12,1,1024,64]{3,2,1,0:T(8,128)(2,1)}, bf16[...) while((s32[]{:T(128)}, ...), condition=%wide.region_4.5_spmd.clone.clone, body=%wide.region_1.4_spmd.clone.sunk.clone | while | flops 287308800 | bytes 13677649 | solution.py:132
  159.8 2.9 multiply_reduce_fusion.3
  165.9 9.2 %fusion.106 = f32[1024,2048]{1,0:T(8,128)} fusion(bf16[1024,768]{0,1:T(8,128)(2,1)} %multiply_convert_fusion.4, bf16[768,2048]{1,0:T(8,128)(2,1)} %all-gather.16.cloned.1.call-done), kind=kOutput, calls=%fused_computation.144 | convolution fusion | flops 3221225472 | bytes 13107200 | tf_op jit(solution)/shard_map/dot_general | solution.py:137
  175.0 10.3 %all-gather.18.cloned.1.call-done = bf16[768,2048]{1,0:T(8,128)(2,1)} async-done(((bf16[96,2048]{1,0:T(8,128)(2,1)}), bf16[768,2048]{1,0:T(8,128)(2,1)}) %all-gather.18.cloned.1.call-update) | async-done | bytes 3145744 | tf_op jit(solution)/shard_map/all_gather | solution.py:72
  185.4 9.2 %fusion.107 = f32[1024,2048]{1,0:T(8,128)} fusion(bf16[1024,768]{0,1:T(8,128)(2,1)} %multiply_convert_fusion.4, bf16[768,2048]{1,0:T(8,128)(2,1)} %all-gather.18.cloned.1.call-done), kind=kOutput, calls=%fused_computation.145 | convolution fusion | flops 3221225472 | bytes 13107200 | tf_op jit(solution)/shard_map/dot_general | solution.py:138
  194.6 29.6 %all-gather.20.cloned.1.call-done = bf16[2048,768]{1,0:T(8,128)(2,1)} async-done(((bf16[256,768]{1,0:T(8,128)(2,1)}), bf16[2048,768]{1,0:T(8,128)(2,1)}) %all-gather.20.cloned.1.call-update) | async-done | bytes 3145744 | tf_op jit(solution)/shard_map/all_gather | solution.py:73
  224.2 14.8 %multiply_convert_fusion.1 = (bf16[1024,2048]{1,0:T(8,128)(2,1)S(1)}, bf16[1024,2048]{1,0:T(8,128)(2,1)}, bf16[1024,2048]{1,0:T(8,128)(2,1)}) fusion(f32[1024,2048]{1,0:T(8,128)} %fusion.106, f32[1024,2048]{1,0:T(8,128)} %fusion.107, bf16[2048,768]{1,0:T(8,128)(2,1)} %all-gather.20.cloned.1.call-done, bf16[1,1024,768]{1,2,0:T(8,128)(2,1)} %copy.54, ...), kind=kOutput, calls=%fused_computation.63 | convolution fusion | flops 3255042048 | bytes 34082816 | tf_op jit(solution)/shard_map/rd,fd->rf/dot_general | solution.py:159
  239.0 7.4 fusion.108
  246.4 4.0 multiply_reduce_fusion.1
  255.8 4.8 convolution_convert_fusion
  260.7 4.3 copy.57
  265.0 149.9 %while.31 = (s32[]{:T(128)}, f32[12,1,1024,64]{2,3,1,0:T(8,128)}, f32[12,1,1024,64]{2,3,1,0:T(8,128)}, bf16[12,1,1024,64]{2,3,1,0:T(8,128)(2,1)S(1)}, bf16[12,1,...) while((s32[]{:T(128)}, f32[12,1,1024,64]{2,3,1,0:T(8,128)}, ...), condition=%wide.region_9.10_spmd.clone.clone, body=%wide.region_7.9_spmd.clone.sunk.clone | while | flops 682753024 | bytes 34105448 | solution.py:214
  267.0 3.2 multiply_reduce_fusion.6
  279.5 3.2 multiply_reduce_fusion.6
  292.0 3.2 multiply_reduce_fusion.6
  304.4 3.2 multiply_reduce_fusion.6
  316.9 3.2 multiply_reduce_fusion.6
  329.3 3.2 multiply_reduce_fusion.6
  341.8 3.2 multiply_reduce_fusion.6
  354.3 3.2 multiply_reduce_fusion.6
  366.8 3.2 multiply_reduce_fusion.6
  379.2 3.2 multiply_reduce_fusion.6
  391.7 3.2 multiply_reduce_fusion.6
  404.2 3.2 multiply_reduce_fusion.6
  414.9 5.0 multiply_add_fusion
  429.8 2.9 fusion.82
  432.8 8.7 %fusion.109 = f32[768,2048]{1,0:T(8,128)} fusion(bf16[1024,768]{0,1:T(8,128)(2,1)} %multiply_convert_fusion.4, bf16[1024,2048]{1,0:T(8,128)(2,1)} %get-tuple-element.260), kind=kOutput, calls=%fused_computation.147 | convolution fusion | flops 3221225472 | bytes 12058624 | tf_op jit(solution)/shard_map/rd,rf->df/dot_general | solution.py:166
  441.8 8.7 %fusion.110 = f32[768,2048]{1,0:T(8,128)} fusion(bf16[1024,768]{0,1:T(8,128)(2,1)} %multiply_convert_fusion.4, bf16[1024,2048]{1,0:T(8,128)(2,1)} %copy-done.30), kind=kOutput, calls=%fused_computation.148 | convolution fusion | flops 3221225472 | bytes 12058624 | tf_op jit(solution)/shard_map/rd,rf->df/dot_general | solution.py:167
  450.6 8.9 %fusion.89 = f32[2048,768]{1,0:T(8,128)} fusion(bf16[1024,2048]{1,0:T(8,128)(2,1)} %get-tuple-element.261, bf16[1,1024,768]{1,2,0:T(8,128)(2,1)} %copy.54, f32[1024]{0:T(1024)S(1)} %fusion.98), kind=kOutput, calls=%fused_computation.125 | convolution fusion | flops 3223584768 | bytes 12062720 | tf_op jit(solution)/shard_map/rf,rd->fd/dot_general | solution.py:158
  460.3 5.0 fusion.112
  465.3 3.0 fusion.111
  471.6 26.8 %reduce-scatter.8.cloned.1.call-done = f32[96,768]{1,0:T(8,128)} async-done(((f32[768,768]{1,0:T(8,128)}), f32[96,768]{1,0:T(8,128)}) %reduce-scatter.8.cloned.1.call-update) | async-done | bytes 294928 | tf_op jit(solution)/shard_map/reduce_scatter | solution.py:249
  500.0 36.7 %reduce-scatter.12.cloned.1.call-done = f32[96,768]{1,0:T(8,128)} async-done(((f32[768,768]{1,0:T(8,128)}), f32[96,768]{1,0:T(8,128)}) %reduce-scatter.12.cloned.1.call-update) | async-done | bytes 294928 | tf_op jit(solution)/shard_map/reduce_scatter | solution.py:251
  538.4 69.1 %reduce-scatter.16.cloned.1.call-done = f32[96,2048]{1,0:T(8,128)} async-done(((f32[768,2048]{1,0:T(8,128)}), f32[96,2048]{1,0:T(8,128)}) %reduce-scatter.16.cloned.1.call-update) | async-done | bytes 786448 | tf_op jit(solution)/shard_map/reduce_scatter | solution.py:253
  609.4 68.6 %reduce-scatter.18.cloned.1.call-done = f32[96,2048]{1,0:T(8,128)} async-done(((f32[768,2048]{1,0:T(8,128)}), f32[96,2048]{1,0:T(8,128)}) %reduce-scatter.18.cloned.1.call-update) | async-done | bytes 786448 | tf_op jit(solution)/shard_map/reduce_scatter | solution.py:254
  679.9 68.4 %reduce-scatter.20.cloned.1.call-done = f32[256,768]{1,0:T(8,128)} async-done(((f32[2048,768]{1,0:T(8,128)}), f32[256,768]{1,0:T(8,128)}) %reduce-scatter.20.cloned.1.call-update) | async-done | bytes 786448 | tf_op jit(solution)/shard_map/reduce_scatter | solution.py:255
  750.3 6.6 fusion.70
  756.9 13.9 %all-reduce.4 = (bf16[768]{0:T(1024)(128)(2,1)S(1)}, bf16[768]{0:T(1024)(128)(2,1)S(1)}) all-reduce(f32[768]{0:T(1024)S(1)} %get-tuple-element.206, f32[768]{0:T(1024)S(1)} %get-tuple-element.204), channel_id=9, replica_groups=mesh['rep'=4,'fsdp'=8] {'fsdp'}, use_global_device_ids=true, to_apply=%region_26.27.clone | all-reduce | flops 1536 | bytes 9216
  771.0 10.5 %all-reduce.6 = (bf16[96]{0:T(256)(128)(2,1)S(1)}, bf16[96]{0:T(256)(128)(2,1)S(1)}) all-reduce(bf16[96]{0:T(256)(128)(2,1)S(1)} %dynamic-slice.9, bf16[96]{0:T(256)(128)(2,1)S(1)} %dynamic-slice.8), channel_id=1, replica_groups=mesh['rep'=4,'fsdp'=8] {'rep'}, use_global_device_ids=true, to_apply=%region_27.28 | all-reduce | flops 192 | bytes 768 | tf_op jit(solution)/shard_map/psum | solution.py:267
  782.5 4.8 fusion.76
  790.1 8.0 fusion.88
  800.7 15.6 %all-reduce.10.cloned.1.call-done = (bf16[96,768]{1,0:T(8,128)(2,1)}, bf16[96,768]{1,0:T(8,128)(2,1)}, bf16[96,768]{1,0:T(8,128)(2,1)}, bf16[96,768]{1,0:T(8,128...) async-done(((bf16[96,768]{1,0:T(8,128)(2,1)}, bf16[96,768]{1,0:T(8,128)(2,1)}, bf16[96,768]{1,0:T(8,128)(2,1)}, ...) | async-done | bytes 1769488 | tf_op jit(solution)/shard_map/psum | solution.py:260
  (285 shorter events, 249.0 us)
Async XLA Ops:
  7.2 31.8 %all-gather.10.cloned.1.call-start = ((), (), s32[]{:S(2)}) async-start(), calls=%async_computation.8 | async-start | bytes 1327104 | tf_op jit(solution)/shard_map/all_gather | solution.py:68
  7.9 51.4 %all-gather.8.cloned.1.call-start = ((), (), s32[]{:S(2)}) async-start(), calls=%async_computation.7 | async-start | bytes 1327104 | tf_op jit(solution)/shard_map/all_gather | solution.py:67
  8.7 74.7 %all-gather.12.cloned.1.call-start = ((), (), s32[]{:S(2)}) async-start(), calls=%async_computation.9 | async-start | bytes 1327104 | tf_op jit(solution)/shard_map/all_gather | solution.py:69
  9.4 150.4 %all-gather.14.cloned.1.call-start = ((), (), s32[]{:S(2)}) async-start(), calls=%async_computation.10 | async-start | bytes 1327104 | tf_op jit(solution)/shard_map/all_gather | solution.py:70
  10.0 155.9 %all-gather.16.cloned.1.call-start = ((), (), s32[]{:S(2)}) async-start(), calls=%async_computation.11 | async-start | bytes 3538944 | tf_op jit(solution)/shard_map/all_gather | solution.py:71
  10.6 174.8 %all-gather.18.cloned.1.call-start = ((), (), s32[]{:S(2)}) async-start(), calls=%async_computation.12 | async-start | bytes 3538944 | tf_op jit(solution)/shard_map/all_gather | solution.py:72
  11.1 213.0 %all-gather.20.cloned.1.call-start = ((), (), s32[]{:S(2)}) async-start(), calls=%async_computation.13 | async-start | bytes 3538944 | tf_op jit(solution)/shard_map/all_gather | solution.py:73
  11.9 456.4 %reduce-scatter.14.cloned.1.call-start = ((), (), s32[]{:S(2)}) async-start(), calls=%async_computation.17 | async-start | bytes 2654208 | tf_op jit(solution)/shard_map/reduce_scatter | solution.py:252
  12.0 2.9 copy-start.25
  12.0 4.2 copy-start.28
  12.0 4.4 copy-start.29
  12.2 24.2 %copy-start = (bf16[12,1,1024,64]{2,3,1,0:T(8,128)(2,1)}, bf16[12,1,1024,64]{2,3,1,0:T(8,128)(2,1)S(1)}, u32[]{:S(2)}) copy-start(bf16[12,1,1024,64]{2,3,1,0:T(8,128)(2,1)S(1)} %fusion.104) | copy-start | bytes 4718596
  14.9 68.5 %copy-start.21 = (f32[1024]{0:T(1024)}, f32[1024]{0:T(1024)S(1)}, u32[]{:S(2)}) copy-start(f32[1024]{0:T(1024)S(1)} %add_rsqrt_fusion.1) | copy-start | bytes 12292
  35.1 48.3 %copy-start.23 = (f32[768]{0:T(1024)}, f32[768]{0:T(1024)S(1)}, u32[]{:S(2)}) copy-start(f32[768]{0:T(1024)S(1)} %convert_element_type.215) | copy-start | bytes 9220
  35.6 29.1 %copy-start.11 = (f32[1024,32]{0,1:T(8,128)}, f32[1024,32]{0,1:T(8,128)S(1)}, u32[]{:S(2)}) copy-start(f32[1024,32]{0,1:T(8,128)S(1)} %get-tuple-element.278) | copy-start | bytes 393220
  35.7 29.1 %copy-start.13 = (f32[1024,32]{0,1:T(8,128)}, f32[1024,32]{0,1:T(8,128)S(1)}, u32[]{:S(2)}) copy-start(f32[1024,32]{0,1:T(8,128)S(1)} %get-tuple-element.279) | copy-start | bytes 393220
  61.7 1.5 copy-start.16
  87.3 4.2 copy-start.2
  162.8 1.6 copy-start.4
  224.2 14.8 %copy-start.26 = (bf16[768,2048]{1,0:T(8,128)(2,1)S(1)}, bf16[768,2048]{1,0:T(8,128)(2,1)}, u32[]{:S(2)}) copy-start(bf16[768,2048]{1,0:T(8,128)(2,1)} %all-gather.16.cloned.1.call-done) | copy-start | bytes 9437188
  239.0 7.4 copy-start.30
  239.0 7.4 copy-start.5
  239.0 7.4 copy-start.27
  246.4 4.0 copy-start.7
  251.3 1.7 copy-start.3
  260.7 4.3 copy-start.1
  264.9 205.0 %reduce-scatter.10.cloned.1.call-start = ((), (), s32[]{:S(2)}) async-start(), calls=%async_computation.15 | async-start | bytes 2654208 | tf_op jit(solution)/shard_map/reduce_scatter | solution.py:250
  265.0 149.9 %copy-start.12 = (f32[1024,32]{0,1:T(8,128)S(1)}, f32[1024,32]{0,1:T(8,128)}, u32[]{:S(2)}) copy-start(f32[1024,32]{0,1:T(8,128)} %copy-done.11) | copy-start | bytes 393220
  265.0 149.9 %copy-start.14 = (f32[1024,32]{0,1:T(8,128)S(1)}, f32[1024,32]{0,1:T(8,128)}, u32[]{:S(2)}) copy-start(f32[1024,32]{0,1:T(8,128)} %copy-done.13) | copy-start | bytes 393220
  419.9 1.3 copy-start.22
  419.9 1.3 copy-start.24
  420.1 1.2 copy-start.8
  424.1 74.3 %reduce-scatter.8.cloned.1.call-start = ((), (), s32[]{:S(2)}) async-start(), calls=%async_computation.14 | async-start | bytes 2654208 | tf_op jit(solution)/shard_map/reduce_scatter | solution.py:249
  425.7 1.1 copy-start.9
  429.7 107.0 %reduce-scatter.12.cloned.1.call-start = ((), (), s32[]{:S(2)}) async-start(), calls=%async_computation.16 | async-start | bytes 2654208 | tf_op jit(solution)/shard_map/reduce_scatter | solution.py:251
  432.7 174.8 %reduce-scatter.16.cloned.1.call-start = ((), (), s32[]{:S(2)}) async-start(), calls=%async_computation.18 | async-start | bytes 7077888 | tf_op jit(solution)/shard_map/reduce_scatter | solution.py:253
  441.5 236.5 %reduce-scatter.18.cloned.1.call-start = ((), (), s32[]{:S(2)}) async-start(), calls=%async_computation.19 | async-start | bytes 7077888 | tf_op jit(solution)/shard_map/reduce_scatter | solution.py:254
  450.6 297.8 %reduce-scatter.20.cloned.1.call-start = ((), (), s32[]{:S(2)}) async-start(), calls=%async_computation.20 | async-start | bytes 7077888 | tf_op jit(solution)/shard_map/reduce_scatter | solution.py:255
  459.5 356.7 %all-reduce.10.cloned.1.call-start = ((), (), s32[]{:S(2)}) async-start(), calls=%async_computation.21 | async-start | bytes 3538944 | tf_op jit(solution)/shard_map/psum | solution.py:260
  460.2 5.1 copy-start.10
  460.3 5.0 copy-start.15
  787.3 2.7 copy-start.6
  816.2 5.9 copy-start.20
  816.2 6.6 copy-start.19
  816.2 7.4 copy-start.18
  816.2 8.1 copy-start.17
Sparse Core Ops, SparseCore 0:
  9.6 25.6 all-gather.9
  37.0 22.2 all-gather.7
  60.9 22.4 all-gather.11
  84.9 22.4 all-gather.13
  108.8 37.8 all-gather.15
  148.2 37.1 all-gather.17
  187.0 37.1 all-gather.19
  265.1 35.9 reduce-scatter.13
  424.2 35.9 reduce-scatter.9
  462.4 35.9 reduce-scatter.7
  500.7 35.9 reduce-scatter.11
  538.9 68.5 reduce-scatter.15
  609.8 68.1 reduce-scatter.17
  680.2 68.1 reduce-scatter.19
  753.3 62.8 all-reduce.9
where the time goes:
time: 844 us; the launch traced here: 832 us
  waiting for transfers between devices  358 us (42%)
  matrix products  299 us (35%)
  other arithmetic  76.5 us (9%)
  blocking collectives  42.9 us (5%)
  local copies, waits for them, and re-layouts  36.6 us (4%)
  between operations  16.9 us (2%)
    reduce_scatter x1, waiting for transfers between devices, local(): lax.psum_scatter(grad_gate, 'fsdp', scatter_dimension=0, tiled=True)  69.1 us
    reduce_scatter x1, waiting for transfers between devices, local(): lax.psum_scatter(grad_up, 'fsdp', scatter_dimension=0, tiled=True)  68.6 us
    reduce_scatter x1, waiting for transfers between devices, local(): lax.psum_scatter(grad_down, 'fsdp', scatter_dimension=0, tiled=True)  68.4 us
    dot_general x12, matrix products, head_backward(): jnp.einsum('sqe,ske->sqk', query_head, key_head, preferred_element_type=j...  38.4 us
    reduce_scatter x1, waiting for transfers between devices, local(): lax.psum_scatter(grad_value, 'fsdp', scatter_dimension=0, tiled=True)  36.7 us
    unnamed x2, blocking collectives  32.4 us
    all_gather x1, waiting for transfers between devices, local(): lax.all_gather(w_down, 'fsdp', axis=0, tiled=True)  29.6 us
    dot_general x12, matrix products, head_backward(): jnp.einsum('sqk,sqe->ske', grad_scores, query_head, preferred_element_typ...  29.3 us
  transfers between devices with their start and end apart: 15, of which 10 were waited for; matrix products, arithmetic and copies ran while one was open for 43% of the time, Pallas kernels for 0%

commit v1 on v0

v1 whole, which is shorter than its diff:
```python
import functools

import jax
import jax.numpy as jnp
import numpy as np
from jax import lax
from jax.experimental import pallas as pl
from jax.experimental.pallas import tpu as pltpu
from jax.sharding import PartitionSpec as P

HEADS = 12
EPSILON = 1e-05
F32 = jnp.float32
BF16 = jnp.bfloat16
NEG = -1e30
VMEM_LIMIT = 56 * 1024 * 1024

NN = (((1,), (0,)), ((), ()))
NT = (((1,), (1,)), ((), ()))


def mm(a, b, dims=NN):
    return lax.dot_general(a, b, dims, preferred_element_type=F32)


def params():
    return pltpu.CompilerParams(
        dimension_semantics=("arbitrary",), vmem_limit_bytes=VMEM_LIMIT
    )


def cost(flops, nbytes, exps=0):
    return pl.CostEstimate(flops=int(flops), bytes_accessed=int(nbytes), transcendentals=int(exps))


def rotary_lanes(seq_length, head_width):
    half = head_width // 2
    inverse = 10000.0 ** (-(np.arange(half, dtype=np.float64) * 2.0 / head_width))
    angles = np.arange(seq_length, dtype=np.float64)[:, None] * inverse[None, :]
    cos = np.cos(angles)
    sin = np.sin(angles)
    return (
        np.concatenate([cos] * 4, axis=1).astype(np.float32),
        np.concatenate([-sin, sin, -sin, sin], axis=1).astype(np.float32),
    )


def turn(y, cos, sin):
    lane = lax.broadcasted_iota(jnp.int32, y.shape, 1)
    first = (lane % 64) < 32
    other = jnp.where(first, pltpu.roll(y, 96, 1), pltpu.roll(y, 32, 1))
    return y * cos + other * sin


def rms_row(x):
    return lax.rsqrt(jnp.mean(x * x, axis=-1, keepdims=True) + EPSILON)


def qkv_body(x_ref, g_ref, w_ref, cos_ref, sin_ref, h_ref, q_ref, k_ref, v_ref):
    x = x_ref[...].astype(F32)
    h = (x * rms_row(x) * g_ref[...].astype(F32)).astype(BF16)
    h_ref[...] = h
    cos = cos_ref[...]
    sin = sin_ref[...]
    for i, out in ((0, q_ref), (1, k_ref)):
        y = mm(h, w_ref[i])
        for c in range(y.shape[1] // 128):
            s = slice(128 * c, 128 * c + 128)
            out[:, s] = turn(y[:, s], cos, sin).astype(BF16)
    v_ref[...] = mm(h, w_ref[2]).astype(BF16)


def qkv_forward(x, gain, wqkv, cos, sin):
    rows, d = x.shape
    rb = 256
    row = pl.BlockSpec((rb, d), lambda i: (i, 0))
    tab = pl.BlockSpec((rb, 128), lambda i: (i, 0))
    out = jax.ShapeDtypeStruct((rows, d), BF16)
    return pl.pallas_call(
        qkv_body,
        grid=(rows // rb,),
        in_specs=[
            row,
            pl.BlockSpec((1, d), lambda i: (0, 0)),
            pl.BlockSpec((3, d, d), lambda i: (0, 0, 0)),
            tab,
            tab,
        ],
        out_specs=[row] * 4,
        out_shape=[out] * 4,
        compiler_params=params(),
        cost_estimate=cost(6 * rows * d * d, 10 * rows * d + 6 * d * d),
        name="qkv",
    )(x, gain, wqkv, cos, sin)


def head_parts(length, q_ref, k_ref, h, q_aug, q_raw, k_aug):
    seq = q_ref.shape[0]
    lane = lax.broadcasted_iota(jnp.int32, (seq, 128), 1)
    row = lax.broadcasted_iota(jnp.int32, (seq, 128), 0)
    mine = (lane // 64) == h
    spare = lane == 64 * (1 - h)
    q = jnp.where(mine, q_ref[...].astype(F32) * 0.125, 0.0)
    if q_raw is not None:
        q_raw[...] = q.astype(BF16)
    q_aug[...] = jnp.where(spare, 1.0, q).astype(BF16)
    mask = jnp.where(spare & (row >= length), NEG, 0.0)
    k_aug[...] = jnp.where(mine, k_ref[...].astype(F32), mask).astype(BF16)


def attn_fwd_body(len_ref, q_ref, k_ref, v_ref, o_ref, lse_ref, q_aug, k_aug, vt, ot):
    length = len_ref[0]
    seq = q_ref.shape[0]
    qb = 256
    vt[...] = v_ref[...].T
    key = lax.broadcasted_iota(jnp.int32, (qb, qb), 0)
    qry = lax.broadcasted_iota(jnp.int32, (qb, qb), 1)
    for h in range(2):
        head_parts(length, q_ref, k_ref, h, q_aug, None, k_aug)
        hs = slice(64 * h, 64 * h + 64)
        for i in range(seq // qb):
            lo, hi = qb * i, qb * i + qb
            q = q_aug[lo:hi, :]
            diag = mm(k_aug[lo:hi, :], q, NT)
            diag = jnp.where(key <= qry, diag, NEG)
            top = jnp.max(diag, axis=0, keepdims=True)
            if lo:
                past = mm(k_aug[:lo, :], q, NT)
                top = jnp.maximum(top, jnp.max(past, axis=0, keepdims=True))
            pd = jnp.exp(diag - top)
            total = jnp.sum(pd, axis=0, keepdims=True)
            acc = mm(vt[hs, lo:hi], pd.astype(BF16))
            if lo:
                pp = jnp.exp(past - top)
                total = total + jnp.sum(pp, axis=0, keepdims=True)
                acc = acc + mm(vt[hs, :lo], pp.astype(BF16))
            ot[hs, lo:hi] = acc / total
            lse_ref[0, h : h + 1, lo:hi] = top + jnp.log(total)
    o_ref[...] = ot[...].T.astype(BF16)


def attention_forward(length, q, k, v):
    seq, d = q.shape
    pairs = d // 128
    col = pl.BlockSpec((seq, 128), lambda p: (0, p))
    return pl.pallas_call(
        attn_fwd_body,
        grid=(pairs,),
        in_specs=[pl.BlockSpec(memory_space=pltpu.SMEM), col, col, col],
        out_specs=[col, pl.BlockSpec((1, 2, seq), lambda p: (p, 0, 0))],
        out_shape=[
            jax.ShapeDtypeStruct((seq, d), BF16),
            jax.ShapeDtypeStruct((pairs, 2, seq), F32),
        ],
        scratch_shapes=[
            pltpu.VMEM((seq, 128), BF16),
            pltpu.VMEM((seq, 128), BF16),
            pltpu.VMEM((128, seq), BF16),
            pltpu.VMEM((128, seq), F32),
        ],
        compiler_params=params(),
        cost_estimate=cost(16 * seq * seq * d, 8 * seq * d, seq * seq * pairs),
        name="attn_fwd",
    )(length, q, k, v)


def attn_bwd_body(
    len_ref, q_ref, k_ref, v_ref, o_ref, go_ref, lse_ref, cos_ref, sin_ref, g_ref,
    qa0, qa1, qz0, qz1, ka0, ka1, gz0, gz1, kt, et, dqt,
):
    length = len_ref[0]
    seq = q_ref.shape[0]
    kb = 256
    qa, qz, ka, gz = (qa0, qa1), (qz0, qz1), (ka0, ka1), (gz0, gz1)
    go = go_ref[...].astype(F32)
    et[...] = (go * o_ref[...].astype(F32)).T
    kt[...] = k_ref[...].T
    lane = lax.broadcasted_iota(jnp.int32, (seq, 128), 1)
    deltas = []
    for h in range(2):
        head_parts(length, q_ref, k_ref, h, qa[h], qz[h], ka[h])
        gz[h][...] = jnp.where((lane // 64) == h, go, 0.0).astype(BF16)
        deltas.append(jnp.sum(et[64 * h : 64 * h + 64, :], axis=0, keepdims=True))
    key = lax.broadcasted_iota(jnp.int32, (kb, kb), 0)
    qry = lax.broadcasted_iota(jnp.int32, (kb, kb), 1)
    causal = key <= qry
    for j in range(seq // kb):
        lo, hi = kb * j, kb * j + kb
        dv = None
        dk = None
        v = v_ref[lo:hi, :]
        for h in range(2):
            hs = slice(64 * h, 64 * h + 64)
            k = ka[h][lo:hi, :]
            parts = [(lo, hi)] + ([(hi, seq)] if hi < seq else [])
            for n, (a, b) in enumerate(parts):
                s = mm(k, qa[h][a:b, :], NT)
                p = jnp.exp(s - lse_ref[0, h : h + 1, a:b])
                if n == 0:
                    p = jnp.where(causal, p, 0.0)
                dp = mm(v, gz[h][a:b, :], NT)
                ds = (p * (dp - deltas[h][:, a:b])).astype(BF16)
                pb = p.astype(BF16)
                tv = mm(pb, gz[h][a:b, :])
                tk = mm(ds, qz[h][a:b, :])
                tq = mm(kt[hs, lo:hi], ds)
                dv = tv if dv is None else dv + tv
                dk = tk if dk is None else dk + tk
                if j == 0:
                    dqt[hs, a:b] = tq
                else:
                    dqt[hs, a:b] += tq
        g_ref[2, lo:hi, :] = dv.astype(BF16)
        g_ref[1, lo:hi, :] = turn(dk, cos_ref[lo:hi, :], -sin_ref[lo:hi, :]).astype(BF16)
    dq = dqt[...].T * 0.125
    g_ref[0] = turn(dq, cos_ref[...], -sin_ref[...]).astype(BF16)


def attention_backward(length, q, k, v, o, go, lse, cos, sin, first, count):
    seq, d = q.shape
    col = pl.BlockSpec((seq, 128), lambda p: (0, p + first))
    tab = pl.BlockSpec((seq, 128), lambda p: (0, 0))
    wide = pltpu.VMEM((seq, 128), BF16)
    return pl.pallas_call(
        attn_bwd_body,
        grid=(count,),
        in_specs=[pl.BlockSpec(memory_space=pltpu.SMEM)]
        + [col] * 5
        + [pl.BlockSpec((1, 2, seq), lambda p: (p + first, 0, 0)), tab, tab],
        out_specs=pl.BlockSpec((3, seq, 128), lambda p: (0, 0, p)),
        out_shape=jax.ShapeDtypeStruct((3, seq, count * 128), BF16),
        scratch_shapes=[wide] * 8
        + [
            pltpu.VMEM((128, seq), BF16),
            pltpu.VMEM((128, seq), F32),
            pltpu.VMEM((128, seq), F32),
        ],
        compiler_params=params(),
        cost_estimate=cost(40 * seq * seq * 128 * count, 16 * seq * 128 * count, seq * seq * count),
        name="attn_bwd",
    )(length, q, k, v, o, go, lse, cos, sin)


def out_body(len_ref, x_ref, o_ref, w_ref, g_ref, ct_ref, x1_ref, h2_ref, gy_ref):
    x1 = x_ref[...].astype(F32) + mm(o_ref[...], w_ref[...])
    x1_ref[...] = x1
    h2_ref[...] = (x1 * rms_row(x1) * g_ref[...].astype(F32)).astype(BF16)
    rb = x1.shape[0]
    row = lax.broadcasted_iota(jnp.int32, x1.shape, 0) + pl.program_id(0) * rb
    gy_ref[...] = jnp.where(row < len_ref[0], ct_ref[...].astype(F32), 0.0).astype(BF16)


def out_forward(length, x, o, w, gain, ct):
    rows, d = x.shape
    rb = 256
    row = pl.BlockSpec((rb, d), lambda i: (i, 0))
    return pl.pallas_call(
        out_body,
        grid=(rows // rb,),
        in_specs=[
            pl.BlockSpec(memory_space=pltpu.SMEM),
            row,
            row,
            pl.BlockSpec((d, d), lambda i: (0, 0)),
            pl.BlockSpec((1, d), lambda i: (0, 0)),
            row,
        ],
        out_specs=[row] * 3,
        out_shape=[
            jax.ShapeDtypeStruct((rows, d), F32),
            jax.ShapeDtypeStruct((rows, d), BF16),
            jax.ShapeDtypeStruct((rows, d), BF16),
        ],
        compiler_params=params(),
        cost_estimate=cost(2 * rows * d * d, 14 * rows * d),
        name="out_fwd",
    )(length, x, o, w, gain, ct)


def ffn_body(h_ref, gy_ref, x1_ref, wg_ref, wu_ref, wd_ref,
             out_ref, gh_ref, gwg_ref, gwu_ref, gwd_ref, ht, acc):
    step = pl.program_id(0)

    @pl.when(step == 0)
    def _():
        ht[...] = h_ref[...].T
        acc[...] = x1_ref[...]
        gh_ref[...] = jnp.zeros_like(gh_ref)

    h = h_ref[...]
    gy = gy_ref[...]
    wg = wg_ref[...]
    wu = wu_ref[...]
    wd = wd_ref[...]
    gate = mm(h, wg)
    up = mm(h, wu)
    g_hidden = mm(gy, wd, NT)
    sig = jax.nn.sigmoid(gate)
    silu = gate * sig
    hidden = (silu * up).astype(BF16)
    g_gate = (g_hidden * up * sig * (1.0 + gate * (1.0 - sig))).astype(BF16)
    g_up = (g_hidden * silu).astype(BF16)
    acc[...] += mm(hidden, wd)
    gwd_ref[...] = mm(hidden.T, gy).astype(BF16)
    gwg_ref[...] = mm(ht[...], g_gate).astype(BF16)
    gwu_ref[...] = mm(ht[...], g_up).astype(BF16)
    gh_ref[...] += mm(g_gate, wg, NT) + mm(g_up, wu, NT)

    @pl.when(step == pl.num_programs(0) - 1)
    def _():
        out_ref[...] = acc[...].astype(BF16)


def ffn(h2, gy, x1, wg, wu, wd):
    rows, d = h2.shape
    width = wg.shape[1]
    fb = 256
    full = pl.BlockSpec((rows, d), lambda i: (0, 0))
    colw = pl.BlockSpec((d, fb), lambda i: (0, i))
    roww = pl.BlockSpec((fb, d), lambda i: (i, 0))
    return pl.pallas_call(
        ffn_body,
        grid=(width // fb,),
        in_specs=[full, full, full, colw, colw, roww],
        out_specs=[full, full, colw, colw, roww],
        out_shape=[
            jax.ShapeDtypeStruct((rows, d), BF16),
            jax.ShapeDtypeStruct((rows, d), F32),
            jax.ShapeDtypeStruct((d, width), BF16),
            jax.ShapeDtypeStruct((d, width), BF16),
            jax.ShapeDtypeStruct((width, d), BF16),
        ],
        scratch_shapes=[pltpu.VMEM((d, rows), BF16), pltpu.VMEM((rows, d), F32)],
        compiler_params=params(),
        cost_estimate=cost(18 * rows * d * width, 14 * rows * d + 12 * d * width, rows * width),
        name="ffn",
    )(h2, gy, x1, wg, wu, wd)


def out_bwd_body(gh_ref, x1_ref, gy_ref, o_ref, w_ref, g_ref,
                 gx_ref, go_ref, gw_ref, gn_ref, acc):
    step = pl.program_id(0)

    @pl.when(step == 0)
    def _():
        acc[...] = jnp.zeros_like(acc)
        gn_ref[...] = jnp.zeros_like(gn_ref)

    x1 = x1_ref[...]
    r = rms_row(x1)
    n = x1 * r
    gh = gh_ref[...]
    gn_ref[...] += jnp.sum(gh * n, axis=0, keepdims=True)
    s = gh * g_ref[...].astype(F32)
    gx = gy_ref[...].astype(F32) + r * (s - n * jnp.mean(s * n, axis=-1, keepdims=True))
    gx_ref[...] = gx
    ga = gx.astype(BF16)
    go_ref[...] = mm(ga, w_ref[...], NT).astype(BF16)
    acc[...] += mm(o_ref[...].T, ga)

    @pl.when(step == pl.num_programs(0) - 1)
    def _():
        gw_ref[...] = acc[...].astype(BF16)


def out_backward(gh, x1, gy, o, w, gain):
    rows, d = x1.shape
    rb = 256
    row = pl.BlockSpec((rb, d), lambda i: (i, 0))
    mat = pl.BlockSpec((d, d), lambda i: (0, 0))
    vec = pl.BlockSpec((1, d), lambda i: (0, 0))
    return pl.pallas_call(
        out_bwd_body,
        grid=(rows // rb,),
        in_specs=[row, row, row, row, mat, vec],
        out_specs=[row, row, mat, vec],
        out_shape=[
            jax.ShapeDtypeStruct((rows, d), F32),
            jax.ShapeDtypeStruct((rows, d), BF16),
            jax.ShapeDtypeStruct((d, d), BF16),
            jax.ShapeDtypeStruct((1, d), F32),
        ],
        scratch_shapes=[pltpu.VMEM((d, d), F32)],
        compiler_params=params(),
        cost_estimate=cost(4 * rows * d * d, 18 * rows * d),
        name="out_bwd",
    )(gh, x1, gy, o, w, gain)


def wgrad_body(h_ref, g_ref, gw_ref, ht):
    @pl.when(pl.program_id(0) == 0)
    def _():
        ht[...] = h_ref[...].T

    gw_ref[0] = mm(ht[...], g_ref[0]).astype(BF16)


def qkv_wgrad(h, g):
    rows, d = h.shape
    width = g.shape[2]
    return pl.pallas_call(
        wgrad_body,
        grid=(3,),
        in_specs=[
            pl.BlockSpec((rows, d), lambda i: (0, 0)),
            pl.BlockSpec((1, rows, width), lambda i: (i, 0, 0)),
        ],
        out_specs=pl.BlockSpec((1, d, width), lambda i: (i, 0, 0)),
        out_shape=jax.ShapeDtypeStruct((3, d, width), BF16),
        scratch_shapes=[pltpu.VMEM((d, rows), BF16)],
        compiler_params=params(),
        cost_estimate=cost(6 * rows * d * width, 8 * rows * d + 6 * d * d),
        name="qkv_wgrad",
    )(h, g)


def qkv_bwd_body(x_ref, gain_ref, w_ref, gx_ref, *refs):
    parts = refs[:-2]
    gi_ref, gn_ref = refs[-2:]

    @pl.when(pl.program_id(0) == 0)
    def _():
        gn_ref[...] = jnp.zeros_like(gn_ref)

    gh = None
    at = 0
    for part in parts:
        width = part.shape[2]
        for i in range(3):
            t = mm(part[i], w_ref[i, :, at : at + width], NT)
            gh = t if gh is None else gh + t
        at += width
    x = x_ref[...].astype(F32)
    r = rms_row(x)
    n = x * r
    gn_ref[...] += jnp.sum(gh * n, axis=0, keepdims=True)
    s = gh * gain_ref[...].astype(F32)
    gx = gx_ref[...] + r * (s - n * jnp.mean(s * n, axis=-1, keepdims=True))
    gi_ref[...] = gx.astype(BF16)


def qkv_backward(x, gain, wqkv, gx, parts):
    rows, d = x.shape
    rb = 256
    row = pl.BlockSpec((rb, d), lambda i: (i, 0))
    vec = pl.BlockSpec((1, d), lambda i: (0, 0))
    return pl.pallas_call(
        qkv_bwd_body,
        grid=(rows // rb,),
        in_specs=[row, vec, pl.BlockSpec((3, d, d), lambda i: (0, 0, 0)), row]
        + [pl.BlockSpec((3, rb, p.shape[2]), lambda i: (0, i, 0)) for p in parts],
        out_specs=[row, vec],
        out_shape=[jax.ShapeDtypeStruct((rows, d), BF16), jax.ShapeDtypeStruct((1, d), F32)],
        compiler_params=params(),
        cost_estimate=cost(6 * rows * d * d, 14 * rows * d),
        name="qkv_bwd",
    )(x, gain, wqkv, gx, *parts)


def local(
    inputs, w_query, w_key, w_value, w_out, w_gate, w_up, w_down, norm_attn, norm_ffn, lengths, cotangent,
):
    seqs, seq, d = inputs.shape
    assert seqs == 1
    x = inputs.reshape(seq, d)
    ct = cotangent.reshape(seq, d)
    cos, sin = (jnp.asarray(t) for t in rotary_lanes(seq, d // HEADS))

    def gather(w):
        return lax.all_gather(w, "fsdp", axis=0, tiled=True)

    gains = lax.all_gather(jnp.stack([norm_attn, norm_ffn]), "fsdp", axis=1, tiled=True)
    gain1 = gains[0:1]
    gain2 = gains[1:2]
    wqkv = lax.all_gather(jnp.stack([w_query, w_key, w_value]), "fsdp", axis=1, tiled=True)
    wo = gather(w_out)
    wg = gather(w_gate)
    wu = gather(w_up)
    wd = gather(w_down)

    h1, q, k, v = qkv_forward(x, gain1, wqkv, cos, sin)
    o, lse = attention_forward(lengths, q, k, v)
    x1, h2, gy = out_forward(lengths, x, o, wo, gain2, ct)
    out, gh2, gwg, gwu, gwd = ffn(h2, gy, x1, wg, wu, wd)
    gx1, go, gwo, gn2 = out_backward(gh2, x1, gy, o, wo, gain2)
    pairs = d // 128
    g = attention_backward(lengths, q, k, v, o, go, lse, cos, sin, 0, pairs)
    gwqkv = qkv_wgrad(h1, g)
    gi, gn1 = qkv_backward(x, gain1, wqkv, gx1, [g])

    def scatter(t, axis):
        return lax.psum_scatter(t, "fsdp", scatter_dimension=axis, tiled=True)

    owned = [scatter(gwqkv, 1), scatter(gwo, 0), scatter(gwg, 0), scatter(gwu, 0), scatter(gwd, 0)]
    owned = lax.psum(tuple(owned), "rep")
    norms = lax.psum(jnp.concatenate([gn1, gn2], axis=0), ("rep", "fsdp"))
    span = norm_attn.shape[0]
    mine = lax.dynamic_slice_in_dim(norms, lax.axis_index("fsdp") * span, span, axis=1)
    gqkv, gwo, gwg, gwu, gwd = (t.astype(F32) for t in owned)
    return (
        out.reshape(inputs.shape),
        gi.reshape(inputs.shape),
        gqkv[0], gqkv[1], gqkv[2],
        gwo, gwg, gwu, gwd,
        mine[0], mine[1],
    )


def solution(mesh):
    rows = P(("rep", "fsdp"), None, None)
    mat = P("fsdp", None)
    vec = P("fsdp")
    return jax.shard_map(
        local,
        mesh=mesh,
        in_specs=(rows,) + (mat,) * 7 + (vec, vec, P(("rep", "fsdp")), rows),
        out_specs=(rows, rows) + (mat,) * 7 + (vec, vec),
        check_vma=False,
    )
```

time: 844 us -> 528 us (0.63); the launches traced: 832 us -> 527 us
  matrix products: 299 us -> 0 us
  Pallas kernels: 0 us -> 136 us
  other arithmetic: 76.5 us -> 7.26 us
  waiting for transfers between devices: 358 us -> 315 us
  local copies, waits for them, and re-layouts: 36.6 us -> 2.23 us
  blocking collectives: 42.9 us -> 52 us
    dot_general x105 -> x0, matrix products: 299 us -> none  [the longest x12 38.4 us: head_backward(): jnp.einsum('sqe,ske->sqk', query_head, key_head, preferred_element_type=j...]
    pallas_call x0 -> x8, Pallas kernels: none -> 136 us  [the longest x1 41.2 us: ffn(): pl.pallas_call(ffn_body, grid=(width // fb,), in_specs=[full, full, full,...]
    reduce_scatter x7 -> x5, waiting for transfers between devices: 270 us -> 162 us  [scatter(): return lax.psum_scatter(t, 'fsdp', scatter_dimension=axis, tiled=True)]
    all_gather x7 -> x5, waiting for transfers between devices: 67.9 us -> 130 us  [the longest x4 102 us: gather(): return lax.all_gather(w, 'fsdp', axis=0, tiled=True)]
    convert_element_type x34 -> x5, other arithmetic: 38.9 us -> 4.69 us  [local(): gqkv, gwo, gwg, gwu, gwd = (t.astype(F32) for t in owned)]
    unnamed x2 -> x0, blocking collectives: 32.4 us -> none
    psum x1, blocking collectives: 10.5 us -> 38.4 us  [local(): norms = lax.psum(jnp.concatenate([gn1, gn2], axis=0), ('rep', 'fsdp'))]
    unnamed x75 -> x15, local copies, waits for them, and re-layouts: 23.9 us -> 0.12 us
  transfers between devices with their start and end apart: 15 -> 11, of which waited for: 10 -> 9; matrix products, arithmetic and copies ran while one was open for 43% -> 0% of each run, Pallas kernels for 0% -> 16%
where the time goes in v1:
time: 528 us; the launch traced here: 527 us
  waiting for transfers between devices  315 us (60%)
  Pallas kernels  136 us (26%)
  blocking collectives  52 us (10%)
  between operations  14.6 us (3%)
  other arithmetic  7.26 us (1%)
    reduce_scatter x5, waiting for transfers between devices, scatter(): return lax.psum_scatter(t, 'fsdp', scatter_dimension=axis, tiled=True)  162 us
    all_gather x4, waiting for transfers between devices, gather(): return lax.all_gather(w, 'fsdp', axis=0, tiled=True)  102 us
    pallas_call x1, Pallas kernels, ffn(): pl.pallas_call(ffn_body, grid=(width // fb,), in_specs=[full, full, full,...  41.2 us
    psum x1, blocking collectives, local(): norms = lax.psum(jnp.concatenate([gn1, gn2], axis=0), ('rep', 'fsdp'))  38.4 us
    pallas_call x1, Pallas kernels, attention_backward(): pl.pallas_call(attn_bwd_body, grid=(count,), in_specs=[pl.BlockSpec(memor...  29.5 us
    all_gather x1, waiting for transfers between devices, local(): lax.all_gather(jnp.stack([w_query, w_key, w_value]), 'fsdp', axis=1, tile...  27.6 us
    pallas_call x1, Pallas kernels, attention_forward(): pl.pallas_call(attn_fwd_body, grid=(pairs,), in_specs=[pl.BlockSpec(memor...  22.7 us
    psum x1, waiting for transfers between devices, local(): owned = lax.psum(tuple(owned), 'rep')  18.4 us
  transfers between devices with their start and end apart: 11, of which 9 were waited for; matrix products, arithmetic and copies ran while one was open for 0% of the time, Pallas kernels for 16%

profile of v1, /device:TPU:0, one launch (start us, length us, event | category | flops | bytes accessed | tf_op | source)
XLA Modules:
  0.0 527.2 jit_solution(8863173456237642640)
XLA Ops:
  7.2 0.0 all-gather.7.cloned.1.call-start
  7.2 1.9 pad_maximum_fusion
  9.1 0.0 all-gather.9.cloned.1.call-start
  9.2 0.7 all-gather.9.cloned.1.call-update
  9.9 0.0 all-gather.11.cloned.1.call-start
  9.9 0.7 all-gather.11.cloned.1.call-update
  10.6 0.0 all-gather.13.cloned.1.call-start
  10.7 0.5 all-gather.13.cloned.1.call-update
  11.2 0.0 all-gather.15.cloned.1.call-start
  11.2 0.5 all-gather.15.cloned.1.call-update
  11.8 0.0 reduce-scatter.8.cloned.1.call-start
  11.9 13.6 %all-gather = bf16[8,96,2]{1,2,0:T(2,128)(2,1)S(1)} all-gather(bf16[1,96,2]{1,2,0:T(2,128)(2,1)S(1)} %maximum_bitcast_fusion), channel_id=1, replica_groups=mesh['rep'=4,'fsdp'=8] {'fsdp'}, dimensions={0}, use_global_device_ids=true | all-gather | bytes 3456 | tf_op jit(solution)/shard_map/all_gather | solution.py:472
  25.4 0.1 reshape.39
  26.2 0.6 fusion
  26.8 27.6 %all-gather.7.cloned.1.call-done.w_ref = bf16[3,768,768]{2,1,0:T(8,128)(2,1)} async-done(((bf16[3,96,768]{2,1,0:T(8,128)(2,1)}), bf16[3,768,768]{2,1,0:T(8,128)(2,1)}) %all-gather.7.cloned.1.call-update) | async-done | bytes 3538960 | tf_op jit(solution)/shard_map/all_gather | solution.py:475
  54.4 8.3 %qkv.1 = (bf16[1024,768]{1,0:T(8,128)(2,1)}, bf16[1024,768]{1,0:T(8,128)(2,1)}, bf16[1024,768]{1,0:T(8,128)(2,1)}, bf16[1024,768]{1,0:T(8,128)(2,1)}) custom-call(bf16[1024,768]{1,0:T(8,128)(2,1)} %bitcast.27, bf16[1,768]{1,0:T(2,128)(2,1)} %get-tuple-element.60.g_ref.gain_ref, bf16[3,768,768]{2,1,0:T(8,128)(2,1)} %all-gather.7.cloned.1.call-done.w_ref, ...), custom_call_target="tpu_custom_call" | custom-call | flops 3623878656 | bytes 11403264 | tf_op jit(solution)/shard_map/qkv/pallas_call | solution.py:79
  62.7 22.7 %attn_fwd.1 = (bf16[1024,768]{1,0:T(8,128)(2,1)}, f32[6,2,1024]{2,1,0:T(2,128)}) custom-call(s32[1]{0:T(128)S(6)} %copy.32.len_ref, bf16[1024,768]{1,0:T(8,128)(2,1)} %get-tuple-element.31.q_ref, bf16[1024,768]{1,0:T(8,128)(2,1)} %get-tuple-element.32.k_ref, bf16[1024,768]{1,0:T(8,128)(2,1)} %get-tuple-element.33.v_ref), custom_call_target="tpu_custom_call" | custom-call | flops 12884901888 | bytes 6291456 | tf_op jit(solution)/shard_map/attn_fwd/pallas_call | solution.py:146
  85.4 7.0 %out_fwd.1 = (f32[1024,768]{1,0:T(8,128)}, bf16[1024,768]{1,0:T(8,128)(2,1)}, bf16[1024,768]{1,0:T(8,128)(2,1)}) custom-call(s32[1]{0:T(128)S(6)} %copy.32.len_ref, bf16[1024,768]{1,0:T(8,128)(2,1)} %bitcast.28, bf16[1024,768]{1,0:T(8,128)(2,1)} %get-tuple-element.34.o_ref, bf16[768,768]{1,0:T(8,128)(2,1)} %all-gather.9.cloned.1.call-done.w_ref, ...), custom_call_target="tpu_custom_call" | custom-call | flops 1207959552 | bytes 11010048 | tf_op jit(solution)/shard_map/out_fwd/pallas_call | solution.py:257
  92.4 24.8 %all-gather.11.cloned.1.call-done.wg_ref = bf16[768,2048]{1,0:T(8,128)(2,1)} async-done(((bf16[96,2048]{1,0:T(8,128)(2,1)}), bf16[768,2048]{1,0:T(8,128)(2,1)}) %all-gather.11.cloned.1.call-update) | async-done | bytes 3145744 | tf_op jit(solution)/shard_map/all_gather | solution.py:470
  117.2 38.6 %all-gather.13.cloned.1.call-done.wu_ref = bf16[768,2048]{1,0:T(8,128)(2,1)} async-done(((bf16[96,2048]{1,0:T(8,128)(2,1)}), bf16[768,2048]{1,0:T(8,128)(2,1)}) %all-gather.13.cloned.1.call-update) | async-done | bytes 3145744 | tf_op jit(solution)/shard_map/all_gather | solution.py:470
  155.9 38.6 %all-gather.15.cloned.1.call-done.wd_ref = bf16[2048,768]{1,0:T(8,128)(2,1)} async-done(((bf16[256,768]{1,0:T(8,128)(2,1)}), bf16[2048,768]{1,0:T(8,128)(2,1)}) %all-gather.15.cloned.1.call-update) | async-done | bytes 3145744 | tf_op jit(solution)/shard_map/all_gather | solution.py:470
  194.5 41.2 %ffn.1 = (bf16[1024,768]{1,0:T(8,128)(2,1)}, f32[1024,768]{1,0:T(8,128)}, bf16[768,2048]{1,0:T(8,128)(2,1)}, bf16[768,2048]{1,0:T(8,128)(2,1)}, bf16[2048,768]{1,0:T(8,128)(2,1)}) custom-call(bf16[1024,768]{1,0:T(8,128)(2,1)} %get-tuple-element.35.h_ref, bf16[1024,768]{1,0:T(8,128)(2,1)} %get-tuple-element.36.gy_ref, f32[1024,768]{1,0:T(8,128)} %get-tuple-element.37.x1_ref, ...), custom_call_target="tpu_custom_call" | custom-call | flops 28991029248 | bytes 29884416 | tf_op jit(solution)/shard_map/ffn/pallas_call | solution.py:321
  235.7 9.5 %out_bwd.1 = (f32[1024,768]{1,0:T(8,128)}, bf16[1024,768]{1,0:T(8,128)(2,1)}, bf16[768,768]{1,0:T(8,128)(2,1)}, f32[1,768]{1,0:T(1,128)}) custom-call(f32[1024,768]{1,0:T(8,128)} %get-tuple-element.39.gh_ref, f32[1024,768]{1,0:T(8,128)} %get-tuple-element.37.x1_ref, bf16[1024,768]{1,0:T(8,128)(2,1)} %get-tuple-element.36.gy_ref, ...), custom_call_target="tpu_custom_call" | custom-call | flops 2415919104 | bytes 14155776 | tf_op jit(solution)/shard_map/out_bwd/pallas_call | solution.py:372
  245.2 0.0 reduce-scatter.10.cloned.1.call-start
  245.3 0.7 reduce-scatter.10.cloned.1.call-update
  246.0 0.0 reduce-scatter.12.cloned.1.call-start
  246.0 0.7 reduce-scatter.12.cloned.1.call-update
  246.8 0.7 reduce-scatter.14.cloned.1.call-update
  247.5 0.2 reduce-scatter.6.cloned.1.call-start
  247.7 29.5 %attn_bwd.1.refs_0_.g_ref = bf16[3,1024,768]{2,1,0:T(8,128)(2,1)} custom-call(s32[1]{0:T(128)S(6)} %copy.32.len_ref, bf16[1024,768]{1,0:T(8,128)(2,1)} %get-tuple-element.31.q_ref, bf16[1024,768]{1,0:T(8,128)(2,1)} %get-tuple-element.32.k_ref, bf16[1024,768]{1,0:T(8,128)(2,1)} %get-tuple-element.33.v_ref, bf16[1024,768]{1,0:T(8,128)(2,1)} %get-tuple-element.34.o_ref, ...), custom_call_target="tpu_custom_call" | custom-call | flops 32212254720 | bytes 12582912 | tf_op jit(solution)/shard_map/attn_bwd/pallas_call | solution.py:224
  277.2 8.0 %qkv_wgrad.1 = bf16[3,768,768]{2,1,0:T(8,128)(2,1)} custom-call(bf16[1024,768]{1,0:T(8,128)(2,1)} %get-tuple-element.44.h_ref, bf16[3,1024,768]{2,1,0:T(8,128)(2,1)} %attn_bwd.1.refs_0_.g_ref), custom_call_target="tpu_custom_call" | custom-call | flops 3623878656 | bytes 9830400 | tf_op jit(solution)/shard_map/qkv_wgrad/pallas_call | solution.py:401
  285.2 0.0 all-reduce.3.cloned.1.call-start
  285.3 33.1 %reduce-scatter.10.cloned.1.call-done = bf16[96,2048]{1,0:T(8,128)(2,1)} async-done(((bf16[768,2048]{1,0:T(8,128)(2,1)}), bf16[96,2048]{1,0:T(8,128)(2,1)}) %reduce-scatter.10.cloned.1.call-update) | async-done | bytes 393232 | tf_op jit(solution)/shard_map/reduce_scatter | solution.py:492
  318.4 41.9 %reduce-scatter.12.cloned.1.call-done = bf16[96,2048]{1,0:T(8,128)(2,1)} async-done(((bf16[768,2048]{1,0:T(8,128)(2,1)}), bf16[96,2048]{1,0:T(8,128)(2,1)}) %reduce-scatter.12.cloned.1.call-update) | async-done | bytes 393232 | tf_op jit(solution)/shard_map/reduce_scatter | solution.py:492
  360.2 42.1 %reduce-scatter.14.cloned.1.call-done = bf16[256,768]{1,0:T(8,128)(2,1)} async-done(((bf16[2048,768]{1,0:T(8,128)(2,1)}), bf16[256,768]{1,0:T(8,128)(2,1)}) %reduce-scatter.14.cloned.1.call-update) | async-done | bytes 393232 | tf_op jit(solution)/shard_map/reduce_scatter | solution.py:492
  402.4 45.1 %reduce-scatter.6.cloned.1.call-done = bf16[3,96,768]{2,1,0:T(8,128)(2,1)} async-done(((bf16[3,768,768]{2,1,0:T(8,128)(2,1)}), bf16[3,96,768]{2,1,0:T(8,128)(2,1)}) %reduce-scatter.6.cloned.1.call-update) | async-done | bytes 442384 | tf_op jit(solution)/shard_map/reduce_scatter | solution.py:492
  447.5 9.4 %qkv_bwd.1 = (bf16[1024,768]{1,0:T(8,128)(2,1)}, f32[1,768]{1,0:T(1,128)}) custom-call(bf16[1024,768]{1,0:T(8,128)(2,1)} %bitcast.29, bf16[1,768]{1,0:T(2,128)(2,1)} %get-tuple-element.60.g_ref.gain_ref, bf16[3,768,768]{2,1,0:T(8,128)(2,1)} %all-gather.7.cloned.1.call-done.w_ref, f32[1024,768]{1,0:T(8,128)} %get-tuple-element.40.gx_ref, ...), custom_call_target="tpu_custom_call" | custom-call | flops 3623878656 | bytes 11010048 | tf_op jit(solution)/shard_map/qkv_bwd/pallas_call | solution.py:447
  456.9 0.7 pad_maximum_fusion.1
  457.6 38.4 %psum.47 = f32[2,768]{1,0:T(2,128)S(1)} all-reduce(f32[2,768]{1,0:T(2,128)S(1)} %pad_maximum_fusion.1), channel_id=1, replica_groups=mesh['rep'=4,'fsdp'=8] {'rep','fsdp'}, use_global_device_ids=true, to_apply=%region_10.0 | all-reduce | flops 1536 | bytes 12288 | tf_op jit(solution)/shard_map/psum | solution.py:496
  496.0 0.1 constant_dynamic-slice_fusion
  496.1 0.5 slice_bitcast_fusion.3
  496.6 18.4 %all-reduce.3.cloned.1.call-done = (bf16[3,96,768]{2,1,0:T(8,128)(2,1)}, bf16[96,768]{1,0:T(8,128)(2,1)}, bf16[96,2048]{1,0:T(8,128)(2,1)}, bf16[96,2048]{1,0:T(8,128)(2,1)}, bf16[256,768]{1,0:T(8,128)(2,1)}) async-done(((bf16[3,96,768]{2,1,0:T(8,128)(2,1)}, bf16[96,768]{1,0:T(8,128)(2,1)}, bf16[96,2048]{1,0:T(8,128)(2,1)}, bf16[96,2048]{1,0:T(8,128)(2,1)}, bf16[256,768]{1,0:T(8,128)(2,1)}), ...) | async-done | bytes 1769488 | tf_op jit(solution)/shard_map/psum | solution.py:495
  515.0 1.1 convert_element_type.15
  516.2 0.9 slice_bitcast_fusion
  517.1 0.9 convert_element_type.17
  518.1 0.9 convert_element_type.18
  519.0 0.9 convert_element_type.19
  520.0 0.7 convert_element_type.16
  (23 shorter events, 0.2 us)
Async XLA Ops:
  7.2 4.7 copy-start.6
  7.2 4.7 copy-start.5
  7.2 47.2 %all-gather.7.cloned.1.call-start = ((), (), s32[]{:S(2)}) async-start(), calls=%async_computation.5 | async-start | bytes 3981312 | tf_op jit(solution)/shard_map/all_gather | solution.py:475
  9.1 76.3 %all-gather.9.cloned.1.call-start = ((), (), s32[]{:S(2)}) async-start(), calls=%async_computation.6 | async-start | bytes 1327104 | tf_op jit(solution)/shard_map/all_gather | solution.py:470
  9.9 107.3 %all-gather.11.cloned.1.call-start = ((), (), s32[]{:S(2)}) async-start(), calls=%async_computation.7 | async-start | bytes 3538944 | tf_op jit(solution)/shard_map/all_gather | solution.py:470
  10.6 145.3 %all-gather.13.cloned.1.call-start = ((), (), s32[]{:S(2)}) async-start(), calls=%async_computation.8 | async-start | bytes 3538944 | tf_op jit(solution)/shard_map/all_gather | solution.py:470
  11.2 183.3 %all-gather.15.cloned.1.call-start = ((), (), s32[]{:S(2)}) async-start(), calls=%async_computation.9 | async-start | bytes 3538944 | tf_op jit(solution)/shard_map/all_gather | solution.py:470
  11.8 273.5 %reduce-scatter.8.cloned.1.call-start = ((), (), s32[]{:S(2)}) async-start(), calls=%async_computation.11 | async-start | bytes 1327104 | tf_op jit(solution)/shard_map/reduce_scatter | solution.py:492
  245.2 73.1 %reduce-scatter.10.cloned.1.call-start = ((), (), s32[]{:S(2)}) async-start(), calls=%async_computation.12 | async-start | bytes 3538944 | tf_op jit(solution)/shard_map/reduce_scatter | solution.py:492
  246.0 114.3 %reduce-scatter.12.cloned.1.call-start = ((), (), s32[]{:S(2)}) async-start(), calls=%async_computation.13 | async-start | bytes 3538944 | tf_op jit(solution)/shard_map/reduce_scatter | solution.py:492
  246.7 155.6 %reduce-scatter.14.cloned.1.call-start = ((), (), s32[]{:S(2)}) async-start(), calls=%async_computation.14 | async-start | bytes 3538944 | tf_op jit(solution)/shard_map/reduce_scatter | solution.py:492
  247.5 200.0 %reduce-scatter.6.cloned.1.call-start = ((), (), s32[]{:S(2)}) async-start(), calls=%async_computation.10 | async-start | bytes 3981312 | tf_op jit(solution)/shard_map/reduce_scatter | solution.py:492
  285.2 229.8 %all-reduce.3.cloned.1.call-start = ((), (), s32[]{:S(2)}) async-start(), calls=%async_computation.15 | async-start | bytes 3538944 | tf_op jit(solution)/shard_map/psum | solution.py:495
  447.5 9.4 %copy-start.4 = (f32[1,768]{1,0:T(1,128)S(1)}, f32[1,768]{1,0:T(1,128)}, u32[]{:S(2)}) copy-start(f32[1,768]{1,0:T(1,128)} %get-tuple-element.50) | copy-start | bytes 9220
  515.0 2.1 copy-start.2
  516.2 1.9 copy-start.1
  517.1 1.9 copy-start
  517.1 2.8 copy-start.3
Sparse Core Ops, SparseCore 0:
  10.2 44.1 all-gather.6
  56.0 21.6 all-gather.8
  79.3 37.8 all-gather.10
  118.7 37.1 all-gather.12
  157.4 37.1 all-gather.14
  245.3 31.8 reduce-scatter.7
  279.6 38.7 reduce-scatter.9
  320.7 39.5 reduce-scatter.11
  362.5 39.7 reduce-scatter.13
  404.5 42.8 reduce-scatter.5
  451.1 63.8 all-reduce.2
